TPU v7x, 32 devices: a whole 2x2x4 slice. The times are simulated.
32 devices in a mesh: term: 8 (over z, core), sector: 4 (over y, x).
Axes of the slice: x: 2, y: 2, z: 4, core: 2. Of those that a mesh axis runs over, the one named last changes fastest.
Arguments:
- wavefunction: bfloat16 [24, 256, 256], P('sector'), may hold values from -6 to 6
- left_env: bfloat16 [24, 24, 256, 256], P('term', 'sector')
- right_env: bfloat16 [24, 24, 256, 256], P('term', 'sector')
- source: int32 [24, 24], P('term'), may hold values from 0 to 23, as said below
- block_size: int32 [24, 2], P('sector'), may hold values from 32 to 256
Outputs:
- first_product: float32 [24, 256, 256], P('sector', 'term')
- second_product: float32 [24, 256, 256], P('sector', 'term')
Inputs may be any that keep to these rules, and one draw needn't show every extreme that they name: Owner of sector s is s // 6. Among the 3 x 6 entries of source in one device's rows (one index of term) and columns (one index of sector), at most 5 name sectors of any one owner, and some owner is named exactly 5 times.
All inputs are finite; a program needn't handle non-finite values.
Results may differ from a plain program's by a relative error of at most 0.0037.
Values may be sent and summed in bfloat16 or wider, within the bound.
A program may use at most 64 MiB of HBM per device.

v0:
```python
import jax
import jax.numpy as jnp
from jax import lax
from jax.sharding import PartitionSpec as P

epsilon = 1e-06


def block_mask(block_size, width):
    positions = jnp.arange(width, dtype=jnp.int32)
    row_keep = positions[None, :] < block_size[:, 0:1]
    column_keep = positions[None, :] < block_size[:, 1:2]
    return row_keep[:, :, None] & column_keep[:, None, :]


def fetch_blocks(masked, source):
    local_count = masked.shape[0]
    width = masked.shape[1]
    bond_count = source.shape[0]
    my_index = lax.axis_index("sector")
    item_count = bond_count * local_count
    wanted = lax.dynamic_slice_in_dim(source, my_index * local_count, local_count, 1).reshape(
        item_count
    )
    pieces = lax.all_gather(masked, "sector", axis=0, tiled=True)
    piece_count = pieces.shape[0]
    numbers = jnp.arange(piece_count, dtype=jnp.int32)
    onehot = (wanted[:, None] == numbers[None, :]).astype(jnp.bfloat16)
    picked = jnp.dot(
        onehot, pieces.reshape(piece_count, width * width), preferred_element_type=jnp.float32
    )
    return picked.astype(jnp.bfloat16).reshape(bond_count, local_count, width, width)


def apply_operator(vector, left_env, right_env, source, keep):
    masked = jnp.where(keep, vector, jnp.zeros_like(vector))
    picked = fetch_blocks(masked, source)
    half_product = jnp.einsum(
        "bkij,bkjl->bkil", left_env, picked, preferred_element_type=jnp.float32
    ).astype(jnp.bfloat16)
    bond_terms = jnp.einsum(
        "bkil,bkml->bkim", half_product, right_env, preferred_element_type=jnp.float32
    )
    summed = jnp.sum(bond_terms, axis=0)
    return (jnp.where(keep, summed, jnp.zeros_like(summed)), masked)


def body(wavefunction, left_env, right_env, source, block_size):
    width = wavefunction.shape[1]
    keep = block_mask(block_size, width)
    term_count = lax.axis_size("term")
    term_index = lax.axis_index("term")
    row_count = width // term_count
    total_count = lax.axis_size("sector") * wavefunction.shape[0] * width * width
    partial_value, masked = apply_operator(wavefunction, left_env, right_env, source, keep)
    masked_float = masked.astype(jnp.float32)
    whole_sum = lax.psum(partial_value, "term")
    first_product = lax.dynamic_slice_in_dim(whole_sum, term_index * row_count, row_count, 1)
    margin, self_norm = lax.psum(
        (jnp.sum(masked_float * whole_sum), jnp.sum(masked_float * masked_float)), "sector"
    )
    residual = whole_sum - margin / self_norm * masked_float
    spread = lax.psum(jnp.sum(residual * residual), "sector")
    next_vector = (residual * lax.rsqrt(spread / total_count + epsilon)).astype(jnp.bfloat16)
    second_partial, _ = apply_operator(next_vector, left_env, right_env, source, keep)
    second_product = lax.psum_scatter(second_partial, "term", scatter_dimension=1, tiled=True)
    return (first_product, second_product)


def solution(mesh):
    placed = (
        P("sector", None, None),
        P("term", "sector", None, None),
        P("term", "sector", None, None),
        P("term", None),
        P("sector", None),
    )
    return jax.shard_map(
        body,
        mesh=mesh,
        in_specs=placed,
        out_specs=(P("sector", "term", None), P("sector", "term", None)),
        check_vma=False,
    )
```

profile of v0, /device:TPU:0, one launch (start us, length us, event | category | flops | bytes accessed | tf_op | source)
XLA Modules:
  0.0 256.0 jit_solution(13237176541998194756)
XLA Ops:
  7.2 0.0 copy-start
  7.2 0.0 copy-start.2
  7.2 0.0 all-gather.3.cloned.1.call-start
  7.2 0.9 slice_bitcast_fusion.1
  8.1 0.1 iota_compare_fusion.3
  8.2 2.3 and_select_fusion.3
  10.5 0.0 all-gather.3.cloned.1.call-update
  10.5 0.0 all-reduce.3.cloned.1.call-start
  10.6 0.0 copy-done.2
  10.6 0.1 constant_dynamic-slice_fusion.1
  10.7 0.1 eq.8
  10.8 46.5 %all-gather.3.cloned.1.call-done = bf16[24,256,256]{2,1,0:T(8,128)(2,1)} async-done(((bf16[6,256,256]{2,1,0:T(8,128)(2,1)}), bf16[24,256,256]{2,1,0:T(8,128)(2,1)}) %all-gather.3.cloned.1.call-update) | async-done | bytes 3145744 | tf_op jit(solution)/shard_map/all_gather | solution.py:25
  57.3 3.7 %copy.16 = bf16[3,8,256,256]{3,1,2,0:T(8,128)(2,1)S(1)} copy(bf16[3,8,256,256]{3,2,1,0:T(8,128)(2,1)} %bitcast.40) | data formatting | bytes 6291456
  60.9 1.0 convolution_convert_fusion.1
  62.0 0.7 copy.17
  62.7 1.7 slice.11
  64.4 0.0 copy-done
  64.4 0.0 copy-start.1
  64.4 5.0 %and_select_fusion.2 = f32[6,256,256]{2,1,0:T(8,128)} fusion(bf16[3,6,256,256]{3,2,1,0:T(8,128)(2,1)S(1)} %copy-done, bf16[3,6,256,256]{3,2,1,0:T(8,128)(2,1)} %bitcast.43, bf16[3,6,256,256]{3,2,1,0:T(8,128)(2,1)} %param.6, pred[6,256]{1,0:T(8,128)(4,1)S(1)} %get-tuple-element.8, pred[6,256]{1,0:T(8,128)(4,1)S(1)} %get-tuple-element.9), kind=kOutput, calls=%fused_computation.4 | convolution fusion | flops 1209925632 | bytes 8653824 | tf_op jit(solution)/shard_map/bkil,bkml->bkim/dot_general | solution.py:41
  69.4 0.0 all-reduce.3.cloned.1.call-update
  69.4 0.0 all-gather.5.cloned.1.call-start
  69.5 62.0 %all-reduce.3.cloned.1.call-done = f32[6,256,256]{2,1,0:T(8,128)} async-done(((f32[6,256,256]{2,1,0:T(8,128)}), f32[6,256,256]{2,1,0:T(8,128)}) %all-reduce.3.cloned.1.call-update) | async-done | bytes 1572880 | tf_op jit(solution)/shard_map/psum | solution.py:57
  131.5 0.0 copy-done.1
  131.5 2.6 %fusion.25 = (f32[]{:T(128)}, f32[]{:T(128)}) fusion(f32[6,256,256]{2,1,0:T(8,128)} %all-reduce.3.cloned.1.call-done, bf16[6,256,256]{2,1,0:T(8,128)(2,1)S(1)} %copy-done.1, pred[6,256]{1,0:T(8,128)(4,1)S(1)} %get-tuple-element.8, pred[6,256]{1,0:T(8,128)(4,1)S(1)} %get-tuple-element.9), kind=kLoop, calls=%fused_computation.24 | loop fusion | flops 2752510 | bytes 2362376 | tf_op jit(solution)/shard_map/reduce_sum | solution.py:60
  134.1 10.4 %all-reduce = (f32[]{:T(128)}, f32[]{:T(128)}) all-reduce(f32[]{:T(128)} %get-tuple-element.3, f32[]{:T(128)} %get-tuple-element.2), channel_id=1, replica_groups=mesh['term'=8,'sector'=4] {'sector'}, use_global_device_ids=true, to_apply=%region_2.3 | all-reduce | flops 2 | bytes 16 | tf_op jit(solution)/shard_map/psum | solution.py:59
  145.9 2.6 %multiply_reduce_fusion = f32[]{:T(128)} fusion(f32[6,256,256]{2,1,0:T(8,128)} %all-reduce.3.cloned.1.call-done, f32[]{:T(128)S(6)} %div.6, bf16[6,256,256]{2,1,0:T(8,128)(2,1)S(1)} %copy-done.1, pred[6,256]{1,0:T(8,128)(4,1)S(1)} %get-tuple-element.8, pred[6,256]{1,0:T(8,128)(4,1)S(1)} %get-tuple-element.9), kind=kLoop, calls=%fused_computation.27 | loop fusion | flops 2752511 | bytes 2362376 | tf_op jit(solution)/shard_map/reduce_sum | solution.py:63
  148.5 8.6 %psum.31 = f32[]{:T(128)} all-reduce(f32[]{:T(128)} %multiply_reduce_fusion), channel_id=1, replica_groups=mesh['term'=8,'sector'=4] {'sector'}, use_global_device_ids=true, to_apply=%region_6.7 | all-reduce | flops 1 | bytes 8 | tf_op jit(solution)/shard_map/psum | solution.py:63
  157.8 2.8 %and_select_fusion.1 = bf16[6,256,256]{2,1,0:T(8,128)(2,1)} fusion(f32[6,256,256]{2,1,0:T(8,128)} %all-reduce.3.cloned.1.call-done, f32[]{:T(128)S(6)} %rsqrt.3, f32[]{:T(128)S(6)} %div.6, pred[6,256]{1,0:T(8,128)(4,1)S(1)} %get-tuple-element.8, pred[6,256]{1,0:T(8,128)(4,1)S(1)} %get-tuple-element.9, bf16[6,256,256]{2,1,0:T(8,128)(2,1)S(1)} %copy-done.1), kind=kLoop, calls=%fused_computation.3 | loop fusion | flops 3145728 | bytes 3148808 | tf_op jit(solution)/shard_map/jit(_where)/select_n | solution.py:36
  160.6 0.0 all-gather.5.cloned.1.call-update
  160.6 0.2 reduce-scatter.2.cloned.1.call-start
  160.8 42.1 %all-gather.5.cloned.1.call-done = bf16[24,256,256]{2,1,0:T(8,128)(2,1)} async-done(((bf16[6,256,256]{2,1,0:T(8,128)(2,1)}), bf16[24,256,256]{2,1,0:T(8,128)(2,1)}) %all-gather.5.cloned.1.call-update) | async-done | bytes 3145744 | tf_op jit(solution)/shard_map/all_gather | solution.py:25
  203.0 3.7 %copy.18 = bf16[3,8,256,256]{3,1,2,0:T(8,128)(2,1)S(1)} copy(bf16[3,8,256,256]{3,2,1,0:T(8,128)(2,1)} %bitcast.41) | data formatting | bytes 6291456
  206.6 1.0 convolution_convert_fusion
  207.7 0.7 copy.19
  208.4 1.7 slice.12
  210.1 4.9 %and_select_fusion = f32[6,256,256]{2,1,0:T(8,128)} fusion(bf16[3,6,256,256]{3,2,1,0:T(8,128)(2,1)S(1)} %copy-done, bf16[3,6,256,256]{3,2,1,0:T(8,128)(2,1)} %bitcast.42, bf16[3,6,256,256]{3,2,1,0:T(8,128)(2,1)} %param.6, pred[6,256]{1,0:T(8,128)(4,1)S(1)} %get-tuple-element.8, pred[6,256]{1,0:T(8,128)(4,1)S(1)} %get-tuple-element.9), kind=kOutput, calls=%fused_computation.2 | convolution fusion | flops 1209925632 | bytes 8653824 | tf_op jit(solution)/shard_map/bkil,bkml->bkim/dot_general | solution.py:41
  215.0 0.0 reduce-scatter.2.cloned.1.call-update
  215.0 1.6 constant_dynamic-slice_fusion
  216.7 32.8 %reduce-scatter.2.cloned.1.call-done = f32[6,32,256]{2,1,0:T(8,128)} async-done(((f32[6,256,256]{2,1,0:T(8,128)}), f32[6,32,256]{2,1,0:T(8,128)}) %reduce-scatter.2.cloned.1.call-update) | async-done | bytes 196624 | tf_op jit(solution)/shard_map/reduce_scatter | solution.py:66
Async XLA Ops:
  7.2 57.2 %copy-start = (bf16[3,6,256,256]{3,2,1,0:T(8,128)(2,1)S(1)}, bf16[3,6,256,256]{3,2,1,0:T(8,128)(2,1)}, u32[]{:S(2)}) copy-start(bf16[3,6,256,256]{3,2,1,0:T(8,128)(2,1)} %param.7) | copy-start | bytes 7077892
  7.2 3.4 %copy-start.2 = (s32[3,24]{1,0:T(4,128)S(1)}, s32[3,24]{1,0:T(4,128)}, u32[]{:S(2)}) copy-start(s32[3,24]{1,0:T(4,128)} %param.8) | copy-start | bytes 868
  7.2 50.1 %all-gather.3.cloned.1.call-start = ((), (), s32[]{:S(2)}) async-start(), calls=%async_computation.1 | async-start | bytes 3932160 | tf_op jit(solution)/shard_map/all_gather | solution.py:25
  10.5 120.9 %all-reduce.3.cloned.1.call-start = ((), (), s32[]{:S(2)}) async-start(), calls=%async_computation.2 | async-start | bytes 3145728 | tf_op jit(solution)/shard_map/psum | solution.py:57
  64.4 67.1 %copy-start.1 = (bf16[6,256,256]{2,1,0:T(8,128)(2,1)S(1)}, bf16[6,256,256]{2,1,0:T(8,128)(2,1)}, u32[]{:S(2)}) copy-start(bf16[6,256,256]{2,1,0:T(8,128)(2,1)} %param.5) | copy-start | bytes 2359300
  69.4 133.6 %all-gather.5.cloned.1.call-start = ((), (), s32[]{:S(2)}) async-start(), calls=%async_computation.3 | async-start | bytes 3932160 | tf_op jit(solution)/shard_map/all_gather | solution.py:25
  160.6 88.8 %reduce-scatter.2.cloned.1.call-start = ((), (), s32[]{:S(2)}) async-start(), calls=%async_computation.4 | async-start | bytes 1769472 | tf_op jit(solution)/shard_map/reduce_scatter | solution.py:66
Sparse Core Ops, SparseCore 0:
  10.7 46.5 all-gather.2
  69.5 61.8 all-reduce.2
  160.7 42.1 all-gather.4
  215.1 34.2 reduce-scatter.1
where the time goes:
time: 256 us
  waiting for transfers between devices  183 us (71%)
  blocking collectives  19 us (7%)
  between operations  15.9 us (6%)
  local copies, waits for them, and re-layouts  14.8 us (6%)
  matrix products  12 us (5%)
  other arithmetic  10.5 us (4%)
    all_gather x2, waiting for transfers between devices, fetch_blocks(): pieces = lax.all_gather(masked, 'sector', axis=0, tiled=True)  88.6 us
    psum x1, waiting for transfers between devices, body(): whole_sum = lax.psum(partial_value, 'term')  62 us
    reduce_scatter x1, waiting for transfers between devices, body(): lax.psum_scatter(second_partial, 'term', scatter_dimension=1, tiled=True)  32.8 us
    unnamed x12, local copies, waits for them, and re-layouts  12.1 us
    psum x1, blocking collectives, body(): lax.psum((jnp.sum(masked_float * whole_sum), jnp.sum(masked_float * maske...  10.4 us
    dot_general x2, matrix products, apply_operator(): jnp.einsum('bkil,bkml->bkim', half_product, right_env, preferred_element_...  9.96 us
    psum x1, blocking collectives, body(): spread = lax.psum(jnp.sum(residual * residual), 'sector')  8.58 us
    select_n x2, other arithmetic, apply_operator(): masked = jnp.where(keep, vector, jnp.zeros_like(vector))  5.17 us
  transfers between devices with their start and end apart: 4, of which 4 were waited for; matrix products, arithmetic and copies ran while one was open for 1% of the time, Pallas kernels for 0%

commit v1 on v0

--- a/solution.py
+++ b/solution.py
@@ -22,7 +22,14 @@
     wanted = lax.dynamic_slice_in_dim(source, my_index * local_count, local_count, 1).reshape(
         item_count
     )
-    pieces = lax.all_gather(masked, "sector", axis=0, tiled=True)
+    ring = [masked]
+    for hop in range(3):
+        ring.append(lax.ppermute(ring[-1], "sector", [(dev, (dev + 1) % 4) for dev in range(4)]))
+    pieces = jnp.roll(
+        jnp.concatenate(ring[::-1], axis=0),
+        (lax.axis_index("sector") + 1) * ring[0].shape[0],
+        axis=0,
+    )
     piece_count = pieces.shape[0]
     numbers = jnp.arange(piece_count, dtype=jnp.int32)
     onehot = (wanted[:, None] == numbers[None, :]).astype(jnp.bfloat16)

time: 256 us -> 279 us (1.090)
  waiting for transfers between devices: 183 us -> 192 us
  other arithmetic: 10.5 us -> 18.7 us
  starting transfers between devices: 0.34 us -> 8.32 us
    ppermute x0 -> x6, waiting for transfers between devices: none -> 99.6 us  [fetch_blocks(): lax.ppermute(ring[-1], 'sector', [(dev, (dev + 1) % 4) for dev in range(4)])]
    all_gather x2 -> x0, waiting for transfers between devices: 88.6 us -> none  [fetch_blocks(): pieces = lax.all_gather(masked, 'sector', axis=0, tiled=True)]
    concatenate x0 -> x2, other arithmetic: none -> 9.97 us  [fetch_blocks(): jnp.roll(jnp.concatenate(ring[::-1], axis=0), (lax.axis_index('sector') +...]
    ppermute x0 -> x6, starting transfers between devices: none -> 8.24 us  [fetch_blocks(): lax.ppermute(ring[-1], 'sector', [(dev, (dev + 1) % 4) for dev in range(4)])]
    unnamed x12, local copies, waits for them, and re-layouts: 12.1 us -> 9.24 us
  transfers between devices with their start and end apart: 4 -> 8, of which waited for: 4 -> 8; matrix products, arithmetic and copies ran while one was open for 1% -> 1% of each run, Pallas kernels for 0% -> 0%
where the time goes in v1:
time: 279 us
  waiting for transfers between devices  192 us (69%)
  blocking collectives  19 us (7%)
  other arithmetic  18.7 us (7%)
  between operations  16.2 us (6%)
  local copies, waits for them, and re-layouts  12.6 us (5%)
  matrix products  12 us (4%)
  starting transfers between devices  8.32 us (3%)
    ppermute x6, waiting for transfers between devices, fetch_blocks(): lax.ppermute(ring[-1], 'sector', [(dev, (dev + 1) % 4) for dev in range(4)])  99.6 us
    psum x1, waiting for transfers between devices, body(): whole_sum = lax.psum(partial_value, 'term')  62 us
    reduce_scatter x1, waiting for transfers between devices, body(): lax.psum_scatter(second_partial, 'term', scatter_dimension=1, tiled=True)  30.4 us
    psum x1, blocking collectives, body(): lax.psum((jnp.sum(masked_float * whole_sum), jnp.sum(masked_float * maske...  10.4 us
    dot_general x2, matrix products, apply_operator(): jnp.einsum('bkil,bkml->bkim', half_product, right_env, preferred_element_...  9.98 us
    concatenate x2, other arithmetic, fetch_blocks(): jnp.roll(jnp.concatenate(ring[::-1], axis=0), (lax.axis_index('sector') +...  9.97 us
    unnamed x12, local copies, waits for them, and re-layouts  9.24 us
    psum x1, blocking collectives, body(): spread = lax.psum(jnp.sum(residual * residual), 'sector')  8.58 us
  transfers between devices with their start and end apart: 8, of which 8 were waited for; matrix products, arithmetic and copies ran while one was open for 1% of the time, Pallas kernels for 0%

profile of v1, /device:TPU:0, one launch (start us, length us, event | category | flops | bytes accessed | tf_op | source)
XLA Modules:
  0.0 278.9 jit_solution(8079701151401976124)
XLA Ops:
  7.2 0.0 copy-start
  7.2 0.0 all-reduce.3.cloned.1.call-start
  7.2 0.9 slice_bitcast_fusion.1
  8.1 0.1 iota_compare_fusion.3
  8.2 1.5 and_select_fusion.3
  9.6 3.0 %collective-permute-start = (bf16[6,256,256]{2,1,0:T(8,128)(2,1)S(1)}, bf16[6,256,256]{2,1,0:T(8,128)(2,1)S(1)}, u32[]{:S(2)}, u32[]{:S(2)}) collective-permute-start(bf16[6,256,256]{2,1,0:T(8,128)(2,1)S(1)} %and_select_fusion.3), channel_id=1, source_target_pairs={{0,1},{1,2},{2,3},{3,0},{4,5},{5,6},{6,7},{7,4},{8,9},{9,10},{10,1... | collective-permute-start | bytes 2359304 | tf_op jit(solution)/shard_map/ppermute | solution.py:27
  12.6 18.5 %collective-permute-done = bf16[6,256,256]{2,1,0:T(8,128)(2,1)S(1)} collective-permute-done((bf16[6,256,256]{2,1,0:T(8,128)(2,1)S(1)}, bf16[6,256,256]{2,1,0:T(8,128)(2,1)S(1)}, u32[]{:S(2)}, u32[]{:S(2)}) %collective-permute-start) | collective-permute-done | bytes 786464 | tf_op jit(solution)/shard_map/ppermute | solution.py:27
  31.1 0.0 copy-start.2
  31.1 0.9 copy-done.2
  32.0 0.8 collective-permute-start.1
  32.8 18.9 %collective-permute-done.1 = bf16[6,256,256]{2,1,0:T(8,128)(2,1)} collective-permute-done((bf16[6,256,256]{2,1,0:T(8,128)(2,1)S(1)}, bf16[6,256,256]{2,1,0:T(8,128)(2,1)}, u32[]{:S(2)}, u32[]{:S(2)}) %collective-permute-start.1) | collective-permute-done | bytes 786464 | tf_op jit(solution)/shard_map/ppermute | solution.py:27
  51.7 0.0 collective-permute-start.2
  51.7 0.8 constant_dynamic-slice_fusion.1
  52.5 0.1 eq.10
  52.6 18.2 %collective-permute-done.2 = bf16[6,256,256]{2,1,0:T(8,128)(2,1)} collective-permute-done((bf16[6,256,256]{2,1,0:T(8,128)(2,1)}, bf16[6,256,256]{2,1,0:T(8,128)(2,1)}, u32[]{:S(2)}, u32[]{:S(2)}) %collective-permute-start.2) | collective-permute-done | bytes 786464 | tf_op jit(solution)/shard_map/ppermute | solution.py:27
  70.8 5.3 %fusion.10 = bf16[24,256,256]{2,1,0:T(8,128)(2,1)S(1)} fusion(s32[]{:T(128)S(6)} %select_n.40, bf16[6,256,256]{2,1,0:T(8,128)(2,1)} %collective-permute-done.2, bf16[6,256,256]{2,1,0:T(8,128)(2,1)} %collective-permute-done.1, bf16[6,256,256]{2,1,0:T(8,128)(2,1)} %copy-done.2, bf16[6,256,256]{2,1,0:T(8,128)(2,1)S(1)} %and_select_fusion.3), kind=kLoop, calls=%fused_computation.28 | loop fusion | flops 11010048 | bytes 6291460 | tf_op jit(solution)/shard_map/jit(_roll_dynamic)/concatenate | solution.py:28
  76.1 1.8 copy.14
  77.9 1.0 convolution_convert_fusion.1
  79.0 0.7 copy.15
  79.7 1.6 slice.11
  81.3 0.0 copy-done
  81.3 0.0 copy-start.1
  81.3 5.0 %and_select_fusion.2 = f32[6,256,256]{2,1,0:T(8,128)} fusion(bf16[3,6,256,256]{3,2,1,0:T(8,128)(2,1)S(1)} %copy-done, bf16[3,6,256,256]{3,2,1,0:T(8,128)(2,1)} %bitcast.43, bf16[3,6,256,256]{3,2,1,0:T(8,128)(2,1)} %param.8, pred[6,256]{1,0:T(8,128)(4,1)S(1)} %get-tuple-element.9, pred[6,256]{1,0:T(8,128)(4,1)S(1)} %get-tuple-element.10), kind=kOutput, calls=%fused_computation.34 | convolution fusion | flops 1209925632 | bytes 8653824 | tf_op jit(solution)/shard_map/bkil,bkml->bkim/dot_general | solution.py:48
  86.3 0.0 all-reduce.3.cloned.1.call-update
  86.4 0.0 reduce-scatter.2.cloned.1.call-start
  86.4 62.0 %all-reduce.3.cloned.1.call-done = f32[6,256,256]{2,1,0:T(8,128)} async-done(((f32[6,256,256]{2,1,0:T(8,128)}), f32[6,256,256]{2,1,0:T(8,128)}) %all-reduce.3.cloned.1.call-update) | async-done | bytes 1572880 | tf_op jit(solution)/shard_map/psum | solution.py:64
  148.4 0.0 copy-done.1
  148.4 2.6 fusion.39
  151.0 10.4 %all-reduce = (f32[]{:T(128)}, f32[]{:T(128)}) all-reduce(f32[]{:T(128)} %get-tuple-element.4, f32[]{:T(128)} %get-tuple-element.3), channel_id=1, replica_groups=mesh['term'=8,'sector'=4] {'sector'}, use_global_device_ids=true, to_apply=%region_2.4 | all-reduce | flops 2 | bytes 16 | tf_op jit(solution)/shard_map/psum | solution.py:66
  162.8 2.6 multiply_reduce_fusion
  165.5 8.6 %psum.31 = f32[]{:T(128)} all-reduce(f32[]{:T(128)} %multiply_reduce_fusion), channel_id=1, replica_groups=mesh['term'=8,'sector'=4] {'sector'}, use_global_device_ids=true, to_apply=%region_6.8 | all-reduce | flops 1 | bytes 8 | tf_op jit(solution)/shard_map/psum | solution.py:70
  174.7 1.9 and_select_fusion.1
  176.7 1.5 collective-permute-start.3
  178.2 16.2 %collective-permute-done.3 = bf16[6,256,256]{2,1,0:T(8,128)(2,1)S(1)} collective-permute-done((bf16[6,256,256]{2,1,0:T(8,128)(2,1)S(1)}, bf16[6,256,256]{2,1,0:T(8,128)(2,1)S(1)}, u32[]{:S(2)}, u32[]{:S(2)}) %collective-permute-start.3) | collective-permute-done | bytes 786464 | tf_op jit(solution)/shard_map/ppermute | solution.py:27
  194.4 1.5 collective-permute-start.4
  195.9 16.2 %collective-permute-done.4 = bf16[6,256,256]{2,1,0:T(8,128)(2,1)S(1)} collective-permute-done((bf16[6,256,256]{2,1,0:T(8,128)(2,1)S(1)}, bf16[6,256,256]{2,1,0:T(8,128)(2,1)S(1)}, u32[]{:S(2)}, u32[]{:S(2)}) %collective-permute-start.4) | collective-permute-done | bytes 786464 | tf_op jit(solution)/shard_map/ppermute | solution.py:27
  212.1 1.5 collective-permute-start.5
  213.6 11.5 %collective-permute-done.5 = bf16[6,256,256]{2,1,0:T(8,128)(2,1)S(1)} collective-permute-done((bf16[6,256,256]{2,1,0:T(8,128)(2,1)S(1)}, bf16[6,256,256]{2,1,0:T(8,128)(2,1)S(1)}, u32[]{:S(2)}, u32[]{:S(2)}) %collective-permute-start.5) | collective-permute-done | bytes 786464 | tf_op jit(solution)/shard_map/ppermute | solution.py:27
  225.1 4.7 %fusion.3 = bf16[24,256,256]{2,1,0:T(8,128)(2,1)S(1)} fusion(s32[]{:T(128)S(6)} %select_n.40, bf16[6,256,256]{2,1,0:T(8,128)(2,1)S(1)} %collective-permute-done.5, bf16[6,256,256]{2,1,0:T(8,128)(2,1)S(1)} %collective-permute-done.4, bf16[6,256,256]{2,1,0:T(8,128)(2,1)S(1)} %collective-permute-done.3, bf16[6,256,256]{2,1,0:T(8,128)(2,1)S(1)} %and_select_fusion.1), kind=kLoop, calls=%fused_computation.21 | loop fusion | flops 11010048 | bytes 6291460 | tf_op jit(solution)/shard_map/jit(_roll_dynamic)/concatenate | solution.py:28
  229.7 1.8 copy.16
  231.6 1.0 convolution_convert_fusion
  232.6 0.7 copy.17
  233.3 1.6 slice.12
  235.0 5.0 %and_select_fusion = f32[6,256,256]{2,1,0:T(8,128)} fusion(bf16[3,6,256,256]{3,2,1,0:T(8,128)(2,1)S(1)} %copy-done, bf16[3,6,256,256]{3,2,1,0:T(8,128)(2,1)} %bitcast.42, bf16[3,6,256,256]{3,2,1,0:T(8,128)(2,1)} %param.8, pred[6,256]{1,0:T(8,128)(4,1)S(1)} %get-tuple-element.9, pred[6,256]{1,0:T(8,128)(4,1)S(1)} %get-tuple-element.10), kind=kOutput, calls=%fused_computation.32 | convolution fusion | flops 1209925632 | bytes 8653824 | tf_op jit(solution)/shard_map/bkil,bkml->bkim/dot_general | solution.py:48
  239.9 0.0 reduce-scatter.2.cloned.1.call-update
  239.9 1.6 constant_dynamic-slice_fusion
  241.6 30.4 %reduce-scatter.2.cloned.1.call-done = f32[6,32,256]{2,1,0:T(8,128)} async-done(((f32[6,256,256]{2,1,0:T(8,128)}), f32[6,32,256]{2,1,0:T(8,128)}) %reduce-scatter.2.cloned.1.call-update) | async-done | bytes 196624 | tf_op jit(solution)/shard_map/reduce_scatter | solution.py:73
Async XLA Ops:
  7.2 74.2 %copy-start = (bf16[3,6,256,256]{3,2,1,0:T(8,128)(2,1)S(1)}, bf16[3,6,256,256]{3,2,1,0:T(8,128)(2,1)}, u32[]{:S(2)}) copy-start(bf16[3,6,256,256]{3,2,1,0:T(8,128)(2,1)} %param.9) | copy-start | bytes 7077892
  7.2 141.2 %all-reduce.3.cloned.1.call-start = ((), (), s32[]{:S(2)}) async-start(), calls=%async_computation.1 | async-start | bytes 3145728 | tf_op jit(solution)/shard_map/psum | solution.py:64
  9.6 21.5 %collective-permute-start = (bf16[6,256,256]{2,1,0:T(8,128)(2,1)S(1)}, bf16[6,256,256]{2,1,0:T(8,128)(2,1)S(1)}, u32[]{:S(2)}, u32[]{:S(2)}) collective-permute-start(bf16[6,256,256]{2,1,0:T(8,128)(2,1)S(1)} %and_select_fusion.3), channel_id=1, source_target_pairs={{0,1},{1,2},{2,3},{3,0},{4,5},{5,6},{6,7},{7,4},{8,9},{9,10},{10,1... | collective-permute-start | bytes 2359304 | tf_op jit(solution)/shard_map/ppermute | solution.py:27
  31.1 0.9 copy-start.2
  32.0 19.7 %collective-permute-start.1 = (bf16[6,256,256]{2,1,0:T(8,128)(2,1)S(1)}, bf16[6,256,256]{2,1,0:T(8,128)(2,1)}, u32[]{:S(2)}, u32[]{:S(2)}) collective-permute-start(bf16[6,256,256]{2,1,0:T(8,128)(2,1)S(1)} %collective-permute-done), channel_id=1, source_target_pairs={{0,1},{1,2},{2,3},{3,0},{4,5},{5,6},{6,7},{7,4},{8,9},{9,10},{10,1... | collective-permute-start | bytes 2359304 | tf_op jit(solution)/shard_map/ppermute | solution.py:27
  51.7 19.1 %collective-permute-start.2 = (bf16[6,256,256]{2,1,0:T(8,128)(2,1)}, bf16[6,256,256]{2,1,0:T(8,128)(2,1)}, u32[]{:S(2)}, u32[]{:S(2)}) collective-permute-start(bf16[6,256,256]{2,1,0:T(8,128)(2,1)} %collective-permute-done.1), channel_id=1, source_target_pairs={{0,1},{1,2},{2,3},{3,0},{4,5},{5,6},{6,7},{7,4},{8,9},{9,10},{10,1... | collective-permute-start | bytes 2359304 | tf_op jit(solution)/shard_map/ppermute | solution.py:27
  81.3 67.1 %copy-start.1 = (bf16[6,256,256]{2,1,0:T(8,128)(2,1)S(1)}, bf16[6,256,256]{2,1,0:T(8,128)(2,1)}, u32[]{:S(2)}) copy-start(bf16[6,256,256]{2,1,0:T(8,128)(2,1)} %param.7) | copy-start | bytes 2359300
  86.4 185.6 %reduce-scatter.2.cloned.1.call-start = ((), (), s32[]{:S(2)}) async-start(), calls=%async_computation.2 | async-start | bytes 1769472 | tf_op jit(solution)/shard_map/reduce_scatter | solution.py:73
  176.7 17.8 %collective-permute-start.3 = (bf16[6,256,256]{2,1,0:T(8,128)(2,1)S(1)}, bf16[6,256,256]{2,1,0:T(8,128)(2,1)S(1)}, u32[]{:S(2)}, u32[]{:S(2)}) collective-permute-start(bf16[6,256,256]{2,1,0:T(8,128)(2,1)S(1)} %and_select_fusion.1), channel_id=1, source_target_pairs={{0,1},{1,2},{2,3},{3,0},{4,5},{5,6},{6,7},{7,4},{8,9},{9,10},{10,1... | collective-permute-start | bytes 2359304 | tf_op jit(solution)/shard_map/ppermute | solution.py:27
  194.4 17.7 %collective-permute-start.4 = (bf16[6,256,256]{2,1,0:T(8,128)(2,1)S(1)}, bf16[6,256,256]{2,1,0:T(8,128)(2,1)S(1)}, u32[]{:S(2)}, u32[]{:S(2)}) collective-permute-start(bf16[6,256,256]{2,1,0:T(8,128)(2,1)S(1)} %collective-permute-done.3), channel_id=1, source_target_pairs={{0,1},{1,2},{2,3},{3,0},{4,5},{5,6},{6,7},{7,4},{8,9},{9,10},{10,1... | collective-permute-start | bytes 2359304 | tf_op jit(solution)/shard_map/ppermute | solution.py:27
  212.1 12.9 %collective-permute-start.5 = (bf16[6,256,256]{2,1,0:T(8,128)(2,1)S(1)}, bf16[6,256,256]{2,1,0:T(8,128)(2,1)S(1)}, u32[]{:S(2)}, u32[]{:S(2)}) collective-permute-start(bf16[6,256,256]{2,1,0:T(8,128)(2,1)S(1)} %collective-permute-done.4), channel_id=1, source_target_pairs={{0,1},{1,2},{2,3},{3,0},{4,5},{5,6},{6,7},{7,4},{8,9},{9,10},{10,1... | collective-permute-start | bytes 2359304 | tf_op jit(solution)/shard_map/ppermute | solution.py:27
Sparse Core Ops, SparseCore 0:
  86.5 61.8 all-reduce.2
  240.1 31.9 reduce-scatter.1
